TPU v7x, 128 devices: a whole 4x4x4 slice. The times are simulated.
128 devices in a mesh: dp: 32 (over x, y, z_hi), pipe: 4 (over z_lo, core).
Axes of the slice: x: 4, y: 4, z: 4 (z_hi: 2, z_lo: 2; z = z_hi * 2 + z_lo), core: 2. Of those that a mesh axis runs over, the one named last changes fastest.
Arguments:
- master: float32 [4, 512, 8192], P('pipe', 'dp'), may hold values from -0.12 to 0.12
- moment1: float32 [4, 512, 8192], P('pipe', 'dp'), may hold values from -3 to 3
- moment2: float32 [4, 512, 8192], P('pipe', 'dp'), may hold values from 0.25 to 4.5
- quant_grad: bfloat16 [4, 512, 8192], P('pipe', 'dp'), may hold values from -120 to 120
- grad_exponent: int32 [4, 512], P('pipe', 'dp'), may hold values from -3 to 2
- replica_params: bfloat16 [4, 32, 512, 8192], P('pipe', 'dp'), as said below
- failed: int32 [4, 2], replicated, may hold values from 0 to 31, as said below
- dest: int32 [4, 512], replicated, may hold values from 0 to 511, as said below
Outputs:
- new_master: float32 [4, 512, 8192], P('pipe', 'dp')
- new_moment1: float32 [4, 512, 8192], P('pipe', 'dp')
- new_moment2: float32 [4, 512, 8192], P('pipe', 'dp')
Inputs may be any that keep to these rules, and one draw needn't show every extreme that they name: `failed`: each group lists 2 distinct ranks; group 0 lists ranks 1 and 16; in every other group some rows of the first listed rank have new positions among the rows of the second listed rank (new position // 16). `dest`: each group's row is a permutation of its rows; the 16 rows of one rank (old rows r * 16 to r * 16 + 15) land in at most 1 row of any one rank's new rows (new position // 16), and some pair of ranks reaches 1 in every group. `replica_params`: within a group the copies of ranks not listed in failed are equal; the copies of listed ranks are zero.
All inputs are finite; a program needn't handle non-finite values.
Results may differ from a plain program's by a relative error of at most 0.0003.
Values may be sent and summed in bfloat16 or wider, within the bound.
A program may use at most 64 MiB of HBM per device.

v0:
```python
import jax
import jax.numpy as jnp
from jax import lax
from jax.sharding import PartitionSpec as P

STEP = 20
beta_one = 0.9
beta_two = 0.95
learn_rate = 0.00015
decay_rate = 0.1
adam_eps = 1e-08
clip_eps = 1e-06


def from_root(value, axis, source):
    kept = jnp.where(lax.axis_index(axis) == source, value, 0).astype(value.dtype)
    return lax.psum(kept, axis)


def adam_step(weights, first, second, grads):
    first_new = beta_one * first + (1.0 - beta_one) * grads
    second_new = beta_two * second + (1.0 - beta_two) * grads * grads
    corr_one = 1.0 - beta_one**STEP
    corr_two = 1.0 - beta_two**STEP
    direction = (
        first_new / corr_one / (jnp.sqrt(second_new / corr_two) + adam_eps) + decay_rate * weights
    )
    return (weights - learn_rate * direction, first_new, second_new)


def local(master, moment1, moment2, quant_grad, grad_exponent, replica_params, failed, dest):
    group_idx = lax.axis_index("pipe")
    my_rank = lax.axis_index("dp")
    ranks_count = lax.axis_size("dp")
    shard_rows = master.shape[1]
    row_width = master.shape[2]
    fail_count = failed.shape[1]
    peer_slots = (shard_rows + ranks_count - 1) // ranks_count
    fail_row = lax.dynamic_index_in_dim(failed, group_idx, 0, keepdims=False)
    dest_row = lax.dynamic_index_in_dim(dest, group_idx, 0, keepdims=False)
    rank_ids = jnp.arange(ranks_count, dtype=jnp.int32)
    is_alive = jnp.all(rank_ids[:, None] != fail_row[None, :], axis=1)
    own_fail = fail_row == my_rank
    is_lost = jnp.any(own_fail)
    copy_rows = replica_params[0, 0]
    first_root = jnp.min(jnp.where(is_alive, rank_ids, ranks_count))
    bf_zero = jnp.zeros((), jnp.bfloat16)
    local_ids = jnp.arange(shard_rows, dtype=jnp.int32)
    group_ids = jnp.arange(dest_row.shape[0], dtype=jnp.int32)
    targets = (dest_row // shard_rows).reshape(ranks_count, shard_rows)
    earlier = local_ids[None, :] < local_ids[:, None]
    same_target = targets[:, :, None] == targets[:, None, :]
    order_in = jnp.sum((same_target & earlier[None, :, :]).astype(jnp.int32), axis=2)
    my_targets = lax.dynamic_index_in_dim(targets, my_rank, 0, keepdims=False)
    my_order = lax.dynamic_index_in_dim(order_in, my_rank, 0, keepdims=False)
    slot_ids = jnp.arange(peer_slots, dtype=jnp.int32)
    pick_mask = (my_targets[None, None, :] == rank_ids[:, None, None]) & (
        my_order[None, None, :] == slot_ids[None, :, None]
    )
    send_index = jnp.sum(jnp.where(pick_mask, local_ids[None, None, :], 0), axis=2).reshape(-1)
    new_rows = my_rank * shard_rows + local_ids
    match_mask = dest_row[None, :] == new_rows[:, None]
    source_row = jnp.sum(jnp.where(match_mask, group_ids[None, :], 0), axis=1)
    source_rank = source_row // shard_rows
    source_order = order_in.reshape(-1)[source_row]
    recv_index = source_rank * peer_slots + source_order
    master_extra = None
    lost_blocks = jnp.stack(
        [
            lax.dynamic_slice_in_dim(copy_rows, fail_row[piece_idx] * shard_rows, shard_rows, 0)
            for piece_idx in range(fail_count)
        ]
    )
    lost_blocks = jnp.where(my_rank == first_root, lost_blocks, bf_zero)
    received_rows = from_root(lost_blocks, "dp", first_root)
    recovered = jnp.sum(
        jnp.where(own_fail[:, None, None], received_rows.astype(jnp.float32), jnp.float32(0.0)),
        axis=0,
    )
    start_master = jnp.where(is_lost, recovered, master[0])
    start_first = jnp.where(is_lost, jnp.float32(0.0), moment1[0])
    start_second = jnp.where(is_lost, jnp.float32(0.0), moment2[0])
    grad = (
        quant_grad[0].astype(jnp.float32) * jnp.exp2(grad_exponent[0].astype(jnp.float32))[:, None]
    )
    grad_total = lax.psum(jnp.sum(grad * grad), ("dp", "pipe"))
    elem_count = lax.axis_size("dp") * lax.axis_size("pipe") * shard_rows * row_width
    clip_scale = jnp.minimum(1.0, 1.0 / jnp.sqrt(grad_total / elem_count + clip_eps))
    clipped = grad * clip_scale

    def to_buffer(values):
        return values[send_index].reshape(ranks_count, peer_slots, row_width)

    w_next, m_next, v_next = adam_step(start_master, start_first, start_second, clipped)
    received = (
        lax.all_to_all(to_buffer(w_next), "dp", split_axis=0, concat_axis=0, tiled=True),
        lax.all_to_all(to_buffer(m_next), "dp", split_axis=0, concat_axis=0, tiled=True),
        lax.all_to_all(to_buffer(v_next), "dp", split_axis=0, concat_axis=0, tiled=True),
    )
    placed = tuple(
        (values.reshape(ranks_count * peer_slots, row_width)[recv_index] for values in received)
    )
    placed_master = placed[0]
    return (placed_master[None], placed[1][None], placed[2][None])


def solution(mesh):
    in_specs = (
        P("pipe", "dp", None),
        P("pipe", "dp", None),
        P("pipe", "dp", None),
        P("pipe", "dp", None),
        P("pipe", "dp"),
        P("pipe", "dp", None, None),
        P(),
        P(),
    )
    out_specs = (P("pipe", "dp", None), P("pipe", "dp", None), P("pipe", "dp", None))
    return jax.shard_map(local, mesh=mesh, in_specs=in_specs, out_specs=out_specs, check_vma=False)
```

profile of v0, /device:TPU:0, one launch (start us, length us, event | category | flops | bytes accessed | tf_op | source)
XLA Modules:
  0.0 445.7 jit_solution(17643683241588214400)
XLA Ops:
  11.3 1.1 dynamic-slice_bitcast_fusion.1
  12.4 0.9 fusion.1
  13.9 1.8 fusion.6
  15.7 69.2 %psum.15 = f32[]{:T(128)} all-reduce(f32[]{:T(128)} %fusion.6), channel_id=1, replica_groups=mesh['dp'=32,'pipe'=4] {'dp','pipe'}, use_global_device_ids=true, to_apply=%region_6.7 | all-reduce | flops 1 | bytes 8 | tf_op jit(solution)/shard_map/psum | solution.py:86
  86.1 1.4 fusion.15
  88.7 277.0 %all-reduce.2.cloned.1.call-done = bf16[2,16,8192]{2,1,0:T(8,128)(2,1)} async-done(((bf16[2,16,8192]{2,1,0:T(8,128)(2,1)}), bf16[2,16,8192]{2,1,0:T(8,128)(2,1)}) %all-reduce.2.cloned.1.call-update) | async-done | bytes 524304 | tf_op jit(solution)/shard_map/psum | solution.py:17
  365.7 1.3 select_reduce_fusion
  367.0 2.7 multiply_subtract_fusion
  369.7 0.9 gather_fusion
  370.6 2.1 copy.22
  372.7 10.0 %all-to-all-start = ((f32[32,1,8192]{2,1,0:T(1,128)}), f32[32,1,8192]{2,1,0:T(1,128)S(1)}, u32[]{:S(2)}, u32[]{:S(2)}) async-start(f32[32,1,8192]{2,1,0:T(1,128)} %copy.22), calls=%async_computation | async-start | bytes 2097152 | tf_op jit(solution)/shard_map/all_to_all | solution.py:96
  382.7 0.9 gather_fusion.3
  383.6 2.1 copy.24
  385.7 12.2 %all-to-all-done = f32[32,1,8192]{2,1,0:T(1,128)S(1)} async-done(((f32[32,1,8192]{2,1,0:T(1,128)}), f32[32,1,8192]{2,1,0:T(1,128)S(1)}, u32[]{:S(2)}, u32[]{:S(2)}) %all-to-all-start) | async-done | bytes 1048608 | tf_op jit(solution)/shard_map/all_to_all | solution.py:96
  397.8 4.7 %all-to-all-start.1 = ((f32[32,1,8192]{2,1,0:T(1,128)}), f32[32,1,8192]{2,1,0:T(1,128)}, u32[]{:S(2)}, u32[]{:S(2)}) async-start(f32[32,1,8192]{2,1,0:T(1,128)} %copy.24), calls=%async_computation.1 | async-start | bytes 2097152 | tf_op jit(solution)/shard_map/all_to_all | solution.py:97
  402.5 0.9 gather_fusion.5
  403.4 2.1 copy.25
  405.5 12.5 %all-to-all-done.1 = f32[32,1,8192]{2,1,0:T(1,128)} async-done(((f32[32,1,8192]{2,1,0:T(1,128)}), f32[32,1,8192]{2,1,0:T(1,128)}, u32[]{:S(2)}, u32[]{:S(2)}) %all-to-all-start.1) | async-done | bytes 1048608 | tf_op jit(solution)/shard_map/all_to_all | solution.py:97
  418.0 3.9 all-to-all-start.2
  423.6 1.5 gather_fusion.2
  425.1 1.8 copy.33
  426.9 1.5 gather_fusion.4
  428.4 8.3 %all-to-all-done.2 = f32[32,1,8192]{2,1,0:T(1,128)S(1)} async-done(((f32[32,1,8192]{2,1,0:T(1,128)}), f32[32,1,8192]{2,1,0:T(1,128)S(1)}, u32[]{:S(2)}, u32[]{:S(2)}) %all-to-all-start.2) | async-done | bytes 1048608 | tf_op jit(solution)/shard_map/all_to_all | solution.py:98
  437.3 1.5 gather_fusion.6
  (30 shorter events, 6.8 us)
Async XLA Ops:
  7.2 358.5 %all-reduce.2.cloned.1.call-start = ((), (), s32[]{:S(2)}) async-start(), calls=%async_computation.3 | async-start | bytes 1048576 | tf_op jit(solution)/shard_map/psum | solution.py:17
  372.7 25.1 %all-to-all-start = ((f32[32,1,8192]{2,1,0:T(1,128)}), f32[32,1,8192]{2,1,0:T(1,128)S(1)}, u32[]{:S(2)}, u32[]{:S(2)}) async-start(f32[32,1,8192]{2,1,0:T(1,128)} %copy.22), calls=%async_computation | async-start | bytes 2097152 | tf_op jit(solution)/shard_map/all_to_all | solution.py:96
  397.8 20.2 %all-to-all-start.1 = ((f32[32,1,8192]{2,1,0:T(1,128)}), f32[32,1,8192]{2,1,0:T(1,128)}, u32[]{:S(2)}, u32[]{:S(2)}) async-start(f32[32,1,8192]{2,1,0:T(1,128)} %copy.24), calls=%async_computation.1 | async-start | bytes 2097152 | tf_op jit(solution)/shard_map/all_to_all | solution.py:97
  418.0 18.7 %all-to-all-start.2 = ((f32[32,1,8192]{2,1,0:T(1,128)}), f32[32,1,8192]{2,1,0:T(1,128)S(1)}, u32[]{:S(2)}, u32[]{:S(2)}) async-start(f32[32,1,8192]{2,1,0:T(1,128)} %copy.25), calls=%async_computation.2 | async-start | bytes 2097152 | tf_op jit(solution)/shard_map/all_to_all | solution.py:98
Sparse Core Ops, SparseCore 0:
  13.4 352.2 all-reduce.1
where the time goes:
time: 446 us
  waiting for transfers between devices  310 us (70%)
  blocking collectives  69.2 us (16%)
  local copies, waits for them, and re-layouts  21.8 us (5%)
  starting transfers between devices  18.6 us (4%)
  between operations  16.8 us (4%)
  other arithmetic  9.3 us (2%)
    psum x1, waiting for transfers between devices, from_root(): return lax.psum(kept, axis)  277 us
    psum x1, blocking collectives, local(): grad_total = lax.psum(jnp.sum(grad * grad), ('dp', 'pipe'))  69.2 us
    all_to_all x1, waiting for transfers between devices, local(): lax.all_to_all(to_buffer(m_next), 'dp', split_axis=0, concat_axis=0, tile...  12.5 us
    all_to_all x1, waiting for transfers between devices, local(): lax.all_to_all(to_buffer(w_next), 'dp', split_axis=0, concat_axis=0, tile...  12.2 us
    all_to_all x1, starting transfers between devices, local(): lax.all_to_all(to_buffer(w_next), 'dp', split_axis=0, concat_axis=0, tile...  9.98 us
  transfers between devices with their start and end apart: 4, of which 4 were waited for; matrix products, arithmetic and copies ran while one was open for 4% of the time, Pallas kernels for 0%

commit v1 on v0

--- a/solution.py
+++ b/solution.py
@@ -14,7 +14,7 @@
 
 def from_root(value, axis, source):
     kept = jnp.where(lax.axis_index(axis) == source, value, 0).astype(value.dtype)
-    return lax.psum(kept, axis)
+    return jnp.sum(lax.all_gather(kept, axis), axis=0)
 
 
 def adam_step(weights, first, second, grads):

time: 446 us -> 265 us (0.59)
  waiting for transfers between devices: 310 us -> 122 us
  other arithmetic: 9.3 us -> 16.5 us
    psum x1 -> x0, waiting for transfers between devices: 277 us -> none  [from_root(): return lax.psum(kept, axis)]
    all_gather x0 -> x1, waiting for transfers between devices: none -> 81.1 us  [from_root(): return jnp.sum(lax.all_gather(kept, axis), axis=0)]
    reduce_sum x0 -> x1, other arithmetic: none -> 8.72 us  [from_root(): return jnp.sum(lax.all_gather(kept, axis), axis=0)]
    all_to_all x1, waiting for transfers between devices: 8.29 us -> 14.2 us  [local(): lax.all_to_all(to_buffer(v_next), 'dp', split_axis=0, concat_axis=0, tile...]
    all_to_all x1, starting transfers between devices: 9.98 us -> 4.11 us  [local(): lax.all_to_all(to_buffer(w_next), 'dp', split_axis=0, concat_axis=0, tile...]
  transfers between devices with their start and end apart: 4 -> 4, of which waited for: 4 -> 4; matrix products, arithmetic and copies ran while one was open for 4% -> 7% of each run, Pallas kernels for 0% -> 0%
where the time goes in v1:
time: 265 us; the launch traced here: 264 us
  waiting for transfers between devices  122 us (46%)
  blocking collectives  72.3 us (27%)
  local copies, waits for them, and re-layouts  21.8 us (8%)
  between operations  16.8 us (6%)
  other arithmetic  16.5 us (6%)
  starting transfers between devices  14.5 us (5%)
    all_gather x1, waiting for transfers between devices, from_root(): return jnp.sum(lax.all_gather(kept, axis), axis=0)  81.1 us
    psum x1, blocking collectives, local(): grad_total = lax.psum(jnp.sum(grad * grad), ('dp', 'pipe'))  72.3 us
    all_to_all x1, waiting for transfers between devices, local(): lax.all_to_all(to_buffer(m_next), 'dp', split_axis=0, concat_axis=0, tile...  15.6 us
    all_to_all x1, waiting for transfers between devices, local(): lax.all_to_all(to_buffer(v_next), 'dp', split_axis=0, concat_axis=0, tile...  14.2 us
    all_to_all x1, waiting for transfers between devices, local(): lax.all_to_all(to_buffer(w_next), 'dp', split_axis=0, concat_axis=0, tile...  11.1 us
    reduce_sum x1, other arithmetic, from_root(): return jnp.sum(lax.all_gather(kept, axis), axis=0)  8.72 us
    reshape x3, local copies, waits for them, and re-layouts, to_buffer(): return values[send_index].reshape(ranks_count, peer_slots, row_width)  6.25 us
    all_to_all x1, starting transfers between devices, local(): lax.all_to_all(to_buffer(m_next), 'dp', split_axis=0, concat_axis=0, tile...  5.72 us
  transfers between devices with their start and end apart: 4, of which 4 were waited for; matrix products, arithmetic and copies ran while one was open for 7% of the time, Pallas kernels for 0%

profile of v1, /device:TPU:0, one launch (start us, length us, event | category | flops | bytes accessed | tf_op | source)
XLA Modules:
  0.0 264.0 jit_solution(16288167504997490529)
XLA Ops:
  7.2 0.9 fusion.19
  11.3 1.1 constant_dynamic-slice_fusion.3
  13.9 1.8 fusion.6
  15.7 72.3 %psum.7 = f32[]{:T(128)} all-reduce(f32[]{:T(128)} %fusion.6), channel_id=1, replica_groups=mesh['dp'=32,'pipe'=4] {'dp','pipe'}, use_global_device_ids=true, to_apply=%region_6.7 | all-reduce | flops 1 | bytes 8 | tf_op jit(solution)/shard_map/psum | solution.py:86
  89.2 1.4 fusion.15
  91.8 81.1 %all-gather.2.cloned.1.call-done = bf16[32,2,16,8192]{3,2,1,0:T(8,128)(2,1)} async-done(((bf16[1,2,16,8192]{3,2,1,0:T(8,128)(2,1)}), bf16[32,2,16,8192]{3,2,1,0:T(8,128)(2,1)}) %all-gather.2.cloned.1.call-update) | async-done | bytes 16777232 | tf_op jit(solution)/shard_map/all_gather | solution.py:17
  172.9 8.7 %reduce_sum.61 = bf16[2,16,8192]{2,1,0:T(8,128)(2,1)S(1)} reduce(bf16[32,2,16,8192]{3,2,1,0:T(8,128)(2,1)} %all-gather.2.cloned.1.call-done, bf16[]{:T(256)} %constant.86.clone.1), dimensions={0}, to_apply=%region_3.4 | reduce | flops 8126464 | bytes 17301506 | tf_op jit(solution)/shard_map/reduce_sum | solution.py:17
  181.9 2.3 multiply_subtract_fusion
  184.2 0.9 gather_fusion.3
  185.1 2.1 copy.24
  187.2 5.7 %all-to-all-start.1 = ((f32[32,1,8192]{2,1,0:T(1,128)}), f32[32,1,8192]{2,1,0:T(1,128)S(1)}, u32[]{:S(2)}, u32[]{:S(2)}) async-start(f32[32,1,8192]{2,1,0:T(1,128)} %copy.24), calls=%async_computation.1 | async-start | bytes 2097152 | tf_op jit(solution)/shard_map/all_to_all | solution.py:97
  192.9 0.9 gather_fusion.5
  193.8 2.1 copy.25
  195.9 15.6 %all-to-all-done.1 = f32[32,1,8192]{2,1,0:T(1,128)S(1)} async-done(((f32[32,1,8192]{2,1,0:T(1,128)}), f32[32,1,8192]{2,1,0:T(1,128)S(1)}, u32[]{:S(2)}, u32[]{:S(2)}) %all-to-all-start.1) | async-done | bytes 1048608 | tf_op jit(solution)/shard_map/all_to_all | solution.py:97
  211.5 4.7 %all-to-all-start.2 = ((f32[32,1,8192]{2,1,0:T(1,128)}), f32[32,1,8192]{2,1,0:T(1,128)}, u32[]{:S(2)}, u32[]{:S(2)}) async-start(f32[32,1,8192]{2,1,0:T(1,128)} %copy.25), calls=%async_computation.2 | async-start | bytes 2097152 | tf_op jit(solution)/shard_map/all_to_all | solution.py:98
  216.2 0.9 gather_fusion
  217.1 2.1 copy.22
  219.2 14.2 %all-to-all-done.2 = f32[32,1,8192]{2,1,0:T(1,128)} async-done(((f32[32,1,8192]{2,1,0:T(1,128)}), f32[32,1,8192]{2,1,0:T(1,128)}, u32[]{:S(2)}, u32[]{:S(2)}) %all-to-all-start.2) | async-done | bytes 1048608 | tf_op jit(solution)/shard_map/all_to_all | solution.py:98
  233.4 4.1 %all-to-all-start = ((f32[32,1,8192]{2,1,0:T(1,128)}), f32[32,1,8192]{2,1,0:T(1,128)S(1)}, u32[]{:S(2)}, u32[]{:S(2)}) async-start(f32[32,1,8192]{2,1,0:T(1,128)} %copy.22), calls=%async_computation | async-start | bytes 2097152 | tf_op jit(solution)/shard_map/all_to_all | solution.py:96
  239.2 1.5 gather_fusion.4
  240.7 1.8 copy.32
  242.5 1.5 gather_fusion.6
  244.0 11.1 %all-to-all-done = f32[32,1,8192]{2,1,0:T(1,128)S(1)} async-done(((f32[32,1,8192]{2,1,0:T(1,128)}), f32[32,1,8192]{2,1,0:T(1,128)S(1)}, u32[]{:S(2)}, u32[]{:S(2)}) %all-to-all-start) | async-done | bytes 1048608 | tf_op jit(solution)/shard_map/all_to_all | solution.py:96
  255.7 1.5 gather_fusion.2
  (37 shorter events, 7.1 us)
Async XLA Ops:
  7.2 165.8 %all-gather.2.cloned.1.call-start = ((), (), s32[]{:S(2)}) async-start(), calls=%async_computation.3 | async-start | bytes 17301504 | tf_op jit(solution)/shard_map/all_gather | solution.py:17
  91.8 90.1 %copy-start = (bf16[1,16,8192]{2,1,0:T(8,128)(2,1)S(1)}, bf16[1,16,8192]{2,1,0:T(8,128)(2,1)}, u32[]{:S(2)}) copy-start(bf16[1,16,8192]{2,1,0:T(8,128)(2,1)} %param.11) | copy-start | bytes 786436
  91.8 90.1 %copy-start.1 = (f32[1,16,8192]{2,1,0:T(8,128)S(1)}, f32[1,16,8192]{2,1,0:T(8,128)}, u32[]{:S(2)}) copy-start(f32[1,16,8192]{2,1,0:T(8,128)} %param.8) | copy-start | bytes 1572868
  91.8 90.1 %copy-start.2 = (f32[1,16,8192]{2,1,0:T(8,128)S(1)}, f32[1,16,8192]{2,1,0:T(8,128)}, u32[]{:S(2)}) copy-start(f32[1,16,8192]{2,1,0:T(8,128)} %param.9) | copy-start | bytes 1572868
  187.2 24.4 %all-to-all-start.1 = ((f32[32,1,8192]{2,1,0:T(1,128)}), f32[32,1,8192]{2,1,0:T(1,128)S(1)}, u32[]{:S(2)}, u32[]{:S(2)}) async-start(f32[32,1,8192]{2,1,0:T(1,128)} %copy.24), calls=%async_computation.1 | async-start | bytes 2097152 | tf_op jit(solution)/shard_map/all_to_all | solution.py:97
  211.5 21.9 %all-to-all-start.2 = ((f32[32,1,8192]{2,1,0:T(1,128)}), f32[32,1,8192]{2,1,0:T(1,128)}, u32[]{:S(2)}, u32[]{:S(2)}) async-start(f32[32,1,8192]{2,1,0:T(1,128)} %copy.25), calls=%async_computation.2 | async-start | bytes 2097152 | tf_op jit(solution)/shard_map/all_to_all | solution.py:98
  233.4 21.7 %all-to-all-start = ((f32[32,1,8192]{2,1,0:T(1,128)}), f32[32,1,8192]{2,1,0:T(1,128)S(1)}, u32[]{:S(2)}, u32[]{:S(2)}) async-start(f32[32,1,8192]{2,1,0:T(1,128)} %copy.22), calls=%async_computation | async-start | bytes 2097152 | tf_op jit(solution)/shard_map/all_to_all | solution.py:96
Sparse Core Ops, SparseCore 0:
  13.4 159.5 all-gather.1
